TPU v7x, 128 devices: a whole 4x4x4 slice. The times are simulated.
128 devices in a mesh: batch: 1, tree: 128 (over z, y, x, core).
Axes of the slice: x: 4, y: 4, z: 4, core: 2. Of those that a mesh axis runs over, the one named last changes fastest.
Arguments:
- x_vecs: float32 [262144, 512], P(('batch', 'tree'))
- d_near: bfloat16 [1024, 256, 256], P('tree')
- u_leaf: bfloat16 [1024, 256, 64], P('tree')
- v_leaf: bfloat16 [1024, 256, 64], P('tree')
- w_h0: bfloat16 [1024, 64, 128], P('tree')
- r_h0: bfloat16 [1024, 64, 128], P('tree')
- b_h0: bfloat16 [1024, 64, 64], P('tree')
- w_h1: bfloat16 [512, 128, 128], P('tree')
- r_h1: bfloat16 [512, 128, 128], P('tree')
- b_h1: bfloat16 [512, 128, 128], P('tree')
- w_h2: bfloat16 [256, 128, 256], P('tree')
- r_h2: bfloat16 [256, 128, 256], P('tree')
- b_h2: bfloat16 [256, 128, 128], P('tree')
- w_upper: bfloat16 [128, 256, 256], P('tree')
- r_upper: bfloat16 [128, 256, 256], P('tree')
- b_upper: bfloat16 [128, 256, 256], P('tree')
- w_top: bfloat16 [124, 256, 256], replicated
- r_top: bfloat16 [124, 256, 256], replicated
- b_top: bfloat16 [126, 256, 256], replicated
Outputs:
- output: float32 [262144, 512], P(('batch', 'tree'))
All inputs are finite; a program needn't handle non-finite values.
Results may differ from a plain program's by a relative error of at most 0.0158533.
Values are sent between devices in bfloat16 or wider.
A program may use at most 1 GiB of HBM per device.

v0:
```python
import math
import jax
import jax.numpy as jnp
from jax import lax
from jax.sharding import PartitionSpec as P


def log_two(count):
    return int(math.log2(count) + 0.5)


def local_blocks(packed):
    depth = log_two(packed.shape[0] + 1)
    return [packed[2 ** step - 1:2 ** (step + 1) - 1] for step in range(depth)]


def merge_local(w_child, x_child):
    prod = jnp.einsum('nkq,nkc->nqc', w_child, x_child, preferred_element_type=jnp.float32)
    pairs = prod.reshape(prod.shape[0] // 2, 2, prod.shape[1], prod.shape[2])
    return (pairs[:, 0] + pairs[:, 1]).astype(jnp.bfloat16)


def couple_local(b_node, x_level):
    pairs = x_level.reshape(x_level.shape[0] // 2, 2, x_level.shape[1], x_level.shape[2])
    swapped = jnp.flip(pairs, axis=1).reshape(x_level.shape)
    return jnp.einsum('nkj,njc->nkc', b_node, swapped, preferred_element_type=jnp.float32)


def push_local(r_child, y_parent, coupled):
    r_pairs = r_child.reshape(r_child.shape[0] // 2, 2, r_child.shape[1], r_child.shape[2])
    prod = jnp.einsum('nekq,nqc->nekc', r_pairs, y_parent, preferred_element_type=jnp.float32)
    return (coupled + prod.reshape(coupled.shape)).astype(jnp.bfloat16)


def pick_node(table, index):
    return lax.dynamic_index_in_dim(table, index, 0, keepdims=False)


def solution(mesh):
    tree_devs = mesh.shape['tree']
    top_depth = log_two(tree_devs)
    rows_spec = P(('batch', 'tree'), None)
    tree_spec = P('tree', None, None)
    full_spec = P(None, None, None)

    def body(x_loc, d_near, u_leaf, v_leaf, w_h0, r_h0, b_h0, w_h1, r_h1, b_h1, w_h2, r_h2, b_h2, w_upper, r_upper, b_upper, w_top, r_top, b_top):
        my_dev = lax.axis_index('tree')
        leaves_dev, leaf_size, leaf_rank = u_leaf.shape
        rhs_cols = x_loc.shape[1]
        x_leaf = x_loc.astype(jnp.bfloat16).reshape(leaves_dev, leaf_size, rhs_cols)
        blocks_w = local_blocks(w_upper)
        blocks_r = local_blocks(r_upper)
        blocks_b = local_blocks(b_upper)
        w_local = [w_h0, w_h1, w_h2] + list(reversed(blocks_w[1:]))
        r_local = [r_h0, r_h1, r_h2] + list(reversed(blocks_r[1:]))
        b_local = [b_h0, b_h1, b_h2] + list(reversed(blocks_b[1:]))
        skel_up = [jnp.einsum('lmk,lmc->lkc', v_leaf, x_leaf, preferred_element_type=jnp.float32).astype(jnp.bfloat16)]
        for w_child in w_local:
            skel_up.append(merge_local(w_child, skel_up[-1]))
        coupled = [couple_local(b_node, x_level) for b_node, x_level in zip(b_local, skel_up[:-1])]
        node_x = skel_up[-1][0]
        own_part = jnp.einsum('kq,kc->qc', blocks_w[0][0], node_x, preferred_element_type=jnp.float32)
        node_idx = my_dev
        step_coupled = []
        for step in range(top_depth):
            stride = 2 ** step
            level = top_depth - step
            pair_list = [(source, source ^ stride) for source in range(tree_devs)]
            sib_x = lax.ppermute(node_x, 'tree', pair_list)
            if step == 0:
                b_here = blocks_b[0][0]
            else:
                b_here = pick_node(b_top, 2 ** level - 2 + node_idx)
            step_coupled.append(jnp.dot(b_here, sib_x, preferred_element_type=jnp.float32))
            if level > 1:
                if step == 0:
                    mine = own_part
                    theirs = lax.ppermute(own_part, 'tree', pair_list)
                else:
                    sib_idx = node_idx + 1 - 2 * (node_idx % 2)
                    mine = jnp.einsum('kq,kc->qc', pick_node(w_top, 2 ** level - 4 + node_idx), node_x, preferred_element_type=jnp.float32)
                    theirs = jnp.einsum('kq,kc->qc', pick_node(w_top, 2 ** level - 4 + sib_idx), sib_x, preferred_element_type=jnp.float32)
                node_x = (mine + theirs).astype(jnp.bfloat16)
                node_idx = node_idx // 2
        y_node = step_coupled[-1].astype(jnp.bfloat16)
        for step in range(top_depth - 2, -1, -1):
            level = top_depth - step
            if step == 0:
                r_here = blocks_r[0][0]
            else:
                r_here = pick_node(r_top, 2 ** level - 4 + my_dev // 2 ** step)
            y_node = (step_coupled[step] + jnp.dot(r_here, y_node, preferred_element_type=jnp.float32)).astype(jnp.bfloat16)
        y_skel = y_node[None]
        for height in range(len(r_local) - 1, -1, -1):
            y_skel = push_local(r_local[height], y_skel, coupled[height])
        near = jnp.einsum('lmj,ljc->lmc', d_near, x_leaf, preferred_element_type=jnp.float32)
        far = jnp.einsum('lmk,lkc->lmc', u_leaf, y_skel, preferred_element_type=jnp.float32)
        return (near + far).reshape(leaves_dev * leaf_size, rhs_cols)

    return jax.shard_map(body, mesh=mesh, in_specs=(rows_spec,) + (tree_spec,) * 15 + (full_spec,) * 3, out_specs=rows_spec, check_vma=False)
```

profile of v0, /device:TPU:1, one launch (start us, length us, event | category | flops | bytes accessed | tf_op | source)
XLA Modules:
  0.0 92.6 jit_solution(10304961348225799501)
XLA Ops:
  0.0 2.6 %convert_element_type.81 = bf16[2048,512]{1,0:T(8,128)(2,1)S(1)} convert(f32[2048,512]{1,0:T(8,128)} %param.19) | non-fusion elementwise | flops 1048576 | bytes 6291456 | tf_op jit(solution)/shard_map/convert_element_type | solution.py:50
  2.6 1.4 %convolution_convert_fusion = bf16[8,64,512]{2,1,0:T(8,128)(2,1)S(1)} fusion(bf16[8,256,64]{1,2,0:T(8,128)(2,1)} %param.22, bf16[8,256,512]{2,1,0:T(8,128)(2,1)S(1)} %bitcast.221), kind=kOutput, calls=%fused_computation.6 | convolution fusion | flops 134479872 | bytes 2883584 | tf_op jit(solution)/shard_map/lmk,lmc->lkc/dot_general | solution.py:57
  4.0 1.6 %fusion.123 = f32[8,512,128]{2,1,0:T(8,128)S(1)} fusion(bf16[8,64,512]{2,1,0:T(8,128)(2,1)S(1)} %convolution_convert_fusion, bf16[8,64,128]{2,1,0:T(8,128)(2,1)} %param.23), kind=kOutput, calls=%fused_computation.130 | convolution fusion | flops 67108864 | bytes 2752512 | tf_op jit(solution)/shard_map/nkq,nkc->nqc/dot_general | solution.py:18
  5.6 0.1 fusion.27
  5.7 0.8 copy-done.1
  6.5 1.2 %fusion.33 = f32[4,512,128]{2,1,0:T(8,128)S(1)} fusion(bf16[4,128,128]{2,1,0:T(8,128)(2,1)} %param.26, bf16[4,1,128,512]{2,3,0,1:T(8,128)(2,1)S(1)} %fusion.27), kind=kOutput, calls=%fused_computation.58 | convolution fusion | flops 67108864 | bytes 1703936 | tf_op jit(solution)/shard_map/nkq,nkc->nqc/dot_general | solution.py:18
  7.8 0.3 convolution_bitcast_fusion
  8.1 0.2 convolution_bitcast_fusion.4
  8.4 1.4 %collective-permute-start.1 = (f32[256,512]{0,1:T(8,128)S(1)}, f32[256,512]{0,1:T(8,128)S(1)}, u32[]{:S(2)}, u32[]{:S(2)}) collective-permute-start(f32[256,512]{0,1:T(8,128)S(1)} %convolution_bitcast_fusion.4), channel_id=1, source_target_pairs={{0,1},{1,0},{2,3},{3,2},{4,5},{5,4},{6,7},{7,6},{8,9},{9,8},{10,11... | collective-permute-start | bytes 1572872 | tf_op jit(solution)/shard_map/ppermute | solution.py:78
  9.8 1.5 %collective-permute-done.1 = f32[256,512]{0,1:T(8,128)S(1)} collective-permute-done((f32[256,512]{0,1:T(8,128)S(1)}, f32[256,512]{0,1:T(8,128)S(1)}, u32[]{:S(2)}, u32[]{:S(2)}) %collective-permute-start.1) | collective-permute-done | bytes 524320 | tf_op jit(solution)/shard_map/ppermute | solution.py:78
  11.3 0.8 add_convert_fusion
  12.1 1.4 %collective-permute-start.2 = (bf16[256,512]{0,1:T(8,128)(2,1)}, bf16[256,512]{0,1:T(8,128)(2,1)}, u32[]{:S(2)}, u32[]{:S(2)}) collective-permute-start(bf16[256,512]{0,1:T(8,128)(2,1)} %add_convert_fusion), channel_id=1, source_target_pairs={{0,2},{1,3},{2,0},{3,1},{4,6},{5,7},{6,4},{7,5},{8,10},{9,11},{10,... | collective-permute-start | bytes 786440 | tf_op jit(solution)/shard_map/ppermute | solution.py:69
  13.4 6.2 %collective-permute-done.2 = bf16[256,512]{0,1:T(8,128)(2,1)} collective-permute-done((bf16[256,512]{0,1:T(8,128)(2,1)}, bf16[256,512]{0,1:T(8,128)(2,1)}, u32[]{:S(2)}, u32[]{:S(2)}) %collective-permute-start.2) | collective-permute-done | bytes 262176 | tf_op jit(solution)/shard_map/ppermute | solution.py:69
  19.7 1.3 %fusion.62 = f32[256,512]{1,0:T(8,128)S(1)} fusion(bf16[256,512]{0,1:T(8,128)(2,1)} %collective-permute-done.2, bf16[124,256,256]{2,1,0:T(8,128)(2,1)} %param.35, s32[]{:T(128)S(6)} %select_n.124), kind=kOutput, calls=%fused_computation.84 | convolution fusion | flops 67108864 | bytes 917508 | tf_op jit(solution)/shard_map/kq,kc->qc/dot_general | solution.py:82
  21.0 2.0 %fusion.8 = bf16[256,512]{1,0:T(8,128)(2,1)} fusion(f32[256,512]{1,0:T(8,128)S(1)} %fusion.62, bf16[256,512]{0,1:T(8,128)(2,1)} %add_convert_fusion, bf16[124,256,256]{2,1,0:T(8,128)(2,1)} %param.35, s32[]{:T(128)S(6)} %select_n.120), kind=kOutput, calls=%fused_computation.28 | convolution fusion | flops 67371008 | bytes 1179652 | tf_op jit(solution)/shard_map/kq,kc->qc/dot_general | solution.py:81
  23.0 2.9 %collective-permute-start.3 = (bf16[256,512]{1,0:T(8,128)(2,1)}, bf16[256,512]{1,0:T(8,128)(2,1)}, u32[]{:S(2)}, u32[]{:S(2)}) collective-permute-start(bf16[256,512]{1,0:T(8,128)(2,1)} %fusion.8), channel_id=1, source_target_pairs={{0,4},{1,5},{2,6},{3,7},{4,0},{5,1},{6,2},{7,3},{8,12},{9,13},{10,... | collective-permute-start | bytes 786440 | tf_op jit(solution)/shard_map/ppermute | solution.py:69
  25.9 1.3 %fusion.57 = f32[256,512]{1,0:T(8,128)S(1)} fusion(bf16[256,512]{1,0:T(8,128)(2,1)} %fusion.8, bf16[124,256,256]{2,1,0:T(8,128)(2,1)} %param.35, s32[]{:T(128)S(6)} %select_n.129), kind=kOutput, calls=%fused_computation.80 | convolution fusion | flops 67108864 | bytes 917508 | tf_op jit(solution)/shard_map/kq,kc->qc/dot_general | solution.py:81
  27.1 4.2 %collective-permute-done.3 = bf16[256,512]{1,0:T(8,128)(2,1)} collective-permute-done((bf16[256,512]{1,0:T(8,128)(2,1)}, bf16[256,512]{1,0:T(8,128)(2,1)}, u32[]{:S(2)}, u32[]{:S(2)}) %collective-permute-start.3) | collective-permute-done | bytes 262176 | tf_op jit(solution)/shard_map/ppermute | solution.py:69
  31.3 2.0 %fusion.10 = bf16[256,512]{1,0:T(8,128)(2,1)} fusion(f32[256,512]{1,0:T(8,128)S(1)} %fusion.57, bf16[256,512]{1,0:T(8,128)(2,1)} %collective-permute-done.3, bf16[124,256,256]{2,1,0:T(8,128)(2,1)} %param.35, s32[]{:T(128)S(6)} %select_n.131), kind=kOutput, calls=%fused_computation.30 | convolution fusion | flops 67371008 | bytes 1179652 | tf_op jit(solution)/shard_map/kq,kc->qc/dot_general | solution.py:82
  33.3 1.4 %collective-permute-start.4 = (bf16[256,512]{1,0:T(8,128)(2,1)}, bf16[256,512]{1,0:T(8,128)(2,1)}, u32[]{:S(2)}, u32[]{:S(2)}) collective-permute-start(bf16[256,512]{1,0:T(8,128)(2,1)} %fusion.10), channel_id=1, source_target_pairs={{0,8},{1,9},{2,10},{3,11},{4,12},{5,13},{6,14},{7,15},{8,0},{9,1},... | collective-permute-start | bytes 786440 | tf_op jit(solution)/shard_map/ppermute | solution.py:69
  34.8 1.3 %fusion.51 = f32[256,512]{1,0:T(8,128)S(1)} fusion(bf16[256,512]{1,0:T(8,128)(2,1)} %fusion.10, bf16[124,256,256]{2,1,0:T(8,128)(2,1)} %param.35, s32[]{:T(128)S(6)} %select_n.136), kind=kOutput, calls=%fused_computation.75 | convolution fusion | flops 67108864 | bytes 917508 | tf_op jit(solution)/shard_map/kq,kc->qc/dot_general | solution.py:81
  36.0 3.1 %collective-permute-done.4 = bf16[256,512]{1,0:T(8,128)(2,1)} collective-permute-done((bf16[256,512]{1,0:T(8,128)(2,1)}, bf16[256,512]{1,0:T(8,128)(2,1)}, u32[]{:S(2)}, u32[]{:S(2)}) %collective-permute-start.4) | collective-permute-done | bytes 262176 | tf_op jit(solution)/shard_map/ppermute | solution.py:69
  39.1 2.0 %fusion.12 = bf16[256,512]{1,0:T(8,128)(2,1)} fusion(f32[256,512]{1,0:T(8,128)S(1)} %fusion.51, bf16[256,512]{1,0:T(8,128)(2,1)} %collective-permute-done.4, bf16[124,256,256]{2,1,0:T(8,128)(2,1)} %param.35, s32[]{:T(128)S(6)} %select_n.138), kind=kOutput, calls=%fused_computation.32 | convolution fusion | flops 67371008 | bytes 1179652 | tf_op jit(solution)/shard_map/kq,kc->qc/dot_general | solution.py:82
  41.1 3.1 %collective-permute-start.5 = (bf16[256,512]{1,0:T(8,128)(2,1)}, bf16[256,512]{1,0:T(8,128)(2,1)}, u32[]{:S(2)}, u32[]{:S(2)}) collective-permute-start(bf16[256,512]{1,0:T(8,128)(2,1)} %fusion.12), channel_id=1, source_target_pairs={{0,16},{1,17},{2,18},{3,19},{4,20},{5,21},{6,22},{7,23},{8,24},{9,... | collective-permute-start | bytes 786440 | tf_op jit(solution)/shard_map/ppermute | solution.py:69
  44.2 1.3 %fusion.45 = f32[256,512]{1,0:T(8,128)S(1)} fusion(bf16[256,512]{1,0:T(8,128)(2,1)} %fusion.12, bf16[124,256,256]{2,1,0:T(8,128)(2,1)} %param.35, s32[]{:T(128)S(6)} %select_n.143), kind=kOutput, calls=%fused_computation.70 | convolution fusion | flops 67108864 | bytes 917508 | tf_op jit(solution)/shard_map/kq,kc->qc/dot_general | solution.py:81
  45.5 2.5 %collective-permute-done.5 = bf16[256,512]{1,0:T(8,128)(2,1)} collective-permute-done((bf16[256,512]{1,0:T(8,128)(2,1)}, bf16[256,512]{1,0:T(8,128)(2,1)}, u32[]{:S(2)}, u32[]{:S(2)}) %collective-permute-start.5) | collective-permute-done | bytes 262176 | tf_op jit(solution)/shard_map/ppermute | solution.py:69
  47.9 2.0 %fusion.14 = bf16[256,512]{1,0:T(8,128)(2,1)} fusion(f32[256,512]{1,0:T(8,128)S(1)} %fusion.45, bf16[256,512]{1,0:T(8,128)(2,1)} %collective-permute-done.5, bf16[124,256,256]{2,1,0:T(8,128)(2,1)} %param.35, s32[]{:T(128)S(6)} %select_n.145), kind=kOutput, calls=%fused_computation.34 | convolution fusion | flops 67371008 | bytes 1179652 | tf_op jit(solution)/shard_map/kq,kc->qc/dot_general | solution.py:82
  49.9 1.7 %collective-permute-start.6 = (bf16[256,512]{1,0:T(8,128)(2,1)}, bf16[256,512]{1,0:T(8,128)(2,1)}, u32[]{:S(2)}, u32[]{:S(2)}) collective-permute-start(bf16[256,512]{1,0:T(8,128)(2,1)} %fusion.14), channel_id=1, source_target_pairs={{0,32},{1,33},{2,34},{3,35},{4,36},{5,37},{6,38},{7,39},{8,40},{9,... | collective-permute-start | bytes 786440 | tf_op jit(solution)/shard_map/ppermute | solution.py:69
  51.6 4.4 %collective-permute-start = (bf16[256,512]{0,1:T(8,128)(2,1)}, bf16[256,512]{0,1:T(8,128)(2,1)}, u32[]{:S(2)}, u32[]{:S(2)}) collective-permute-start(bf16[256,512]{0,1:T(8,128)(2,1)} %copy-done.3), channel_id=1, source_target_pairs={{0,1},{1,0},{2,3},{3,2},{4,5},{5,4},{6,7},{7,6},{8,9},{9,8},{10,11... | collective-permute-start | bytes 786440 | tf_op jit(solution)/shard_map/ppermute | solution.py:69
  56.0 0.7 reshape.76
  56.7 1.9 %rev.11 = bf16[2,2,128,512]{2,3,1,0:T(8,128)(2,1)} reverse(bf16[2,2,128,512]{2,3,1,0:T(8,128)(2,1)} %bitcast.224), dimensions={1} | reverse | bytes 1048576 | tf_op jit(solution)/shard_map/jit(_flip)/rev | solution.py:25
  58.6 1.9 %rev.10 = bf16[4,2,64,512]{3,2,1,0:T(8,128)(2,1)} reverse(bf16[4,2,64,512]{3,2,1,0:T(8,128)(2,1)} %bitcast.225), dimensions={1} | reverse | bytes 1048576 | tf_op jit(solution)/shard_map/jit(_flip)/rev | solution.py:25
  60.5 1.3 %fusion.39 = f32[256,512]{1,0:T(8,128)S(1)} fusion(bf16[256,512]{1,0:T(8,128)(2,1)} %fusion.14, bf16[124,256,256]{2,1,0:T(8,128)(2,1)} %param.35, s32[]{:T(128)S(6)} %select_n.150), kind=kOutput, calls=%fused_computation.65 | convolution fusion | flops 67108864 | bytes 917508 | tf_op jit(solution)/shard_map/kq,kc->qc/dot_general | solution.py:81
  61.8 1.3 %fusion.16 = bf16[256,512]{1,0:T(8,128)(2,1)S(1)} fusion(f32[256,512]{1,0:T(8,128)S(1)} %fusion.39, bf16[256,512]{1,0:T(8,128)(2,1)} %collective-permute-done.6, bf16[124,256,256]{2,1,0:T(8,128)(2,1)} %param.35, s32[]{:T(128)S(6)} %select_n.152), kind=kOutput, calls=%fused_computation.36 | convolution fusion | flops 67371008 | bytes 1179652 | tf_op jit(solution)/shard_map/kq,kc->qc/dot_general | solution.py:82
  63.1 3.4 %collective-permute-start.7 = (bf16[256,512]{1,0:T(8,128)(2,1)S(1)}, bf16[256,512]{1,0:T(8,128)(2,1)}, u32[]{:S(2)}, u32[]{:S(2)}) collective-permute-start(bf16[256,512]{1,0:T(8,128)(2,1)S(1)} %fusion.16), channel_id=1, source_target_pairs={{0,64},{1,65},{2,66},{3,67},{4,68},{5,69},{6,70},{7,71},{8,72},{9,... | collective-permute-start | bytes 786440 | tf_op jit(solution)/shard_map/ppermute | solution.py:69
  66.5 2.7 %fusion.122 = f32[8,256,512]{2,1,0:T(8,128)} fusion(bf16[8,256,256]{2,1,0:T(8,128)(2,1)S(1)} %copy-done, bf16[8,256,512]{2,1,0:T(8,128)(2,1)S(1)} %bitcast.222), kind=kOutput, calls=%fused_computation.129 | convolution fusion | flops 536870912 | bytes 7340032 | tf_op jit(solution)/shard_map/lmj,ljc->lmc/dot_general | solution.py:96
  69.2 4.1 %collective-permute-done.7 = bf16[256,512]{1,0:T(8,128)(2,1)} collective-permute-done((bf16[256,512]{1,0:T(8,128)(2,1)S(1)}, bf16[256,512]{1,0:T(8,128)(2,1)}, u32[]{:S(2)}, u32[]{:S(2)}) %collective-permute-start.7) | collective-permute-done | bytes 262176 | tf_op jit(solution)/shard_map/ppermute | solution.py:69
  73.3 1.5 %fusion.20 = f32[256,512]{1,0:T(8,128)S(1)} fusion(bf16[256,512]{1,0:T(8,128)(2,1)} %collective-permute-done.7, bf16[126,256,256]{2,1,0:T(8,128)(2,1)} %param.37, s32[]{:T(128)S(6)} %select_n.149, bf16[124,256,256]{2,1,0:T(8,128)(2,1)} %param.36, s32[]{:T(128)S(6)} %select_n.147), kind=kOutput, calls=%fused_computation.40 | convolution fusion | flops 134348800 | bytes 1048584 | tf_op jit(solution)/shard_map/dot_general | solution.py:92
  74.8 1.5 %fusion.21 = f32[256,512]{1,0:T(8,128)S(1)} fusion(f32[256,512]{1,0:T(8,128)S(1)} %fusion.20, bf16[256,512]{1,0:T(8,128)(2,1)} %collective-permute-done.6, bf16[126,256,256]{2,1,0:T(8,128)(2,1)} %param.37, s32[]{:T(128)S(6)} %select_n.142, bf16[124,256,256]{2,1,0:T(8,128)(2,1)} %param.36, s32[]{:T(128)S(6)} %select_n.140), kind=kOutput, calls=%fused_computation.41 | convolution fusion | flops 134479872 | bytes 1572872 | tf_op jit(solution)/shard_map/dot_general | solution.py:92
  76.3 1.5 %fusion.22 = f32[256,512]{1,0:T(8,128)S(1)} fusion(f32[256,512]{1,0:T(8,128)S(1)} %fusion.21, bf16[256,512]{1,0:T(8,128)(2,1)} %collective-permute-done.5, bf16[126,256,256]{2,1,0:T(8,128)(2,1)} %param.37, s32[]{:T(128)S(6)} %select_n.135, bf16[124,256,256]{2,1,0:T(8,128)(2,1)} %param.36, s32[]{:T(128)S(6)} %select_n.133), kind=kOutput, calls=%fused_computation.42 | convolution fusion | flops 134479872 | bytes 1572872 | tf_op jit(solution)/shard_map/dot_general | solution.py:92
  77.8 1.5 %fusion.23 = f32[256,512]{1,0:T(8,128)S(1)} fusion(f32[256,512]{1,0:T(8,128)S(1)} %fusion.22, bf16[256,512]{1,0:T(8,128)(2,1)} %collective-permute-done.4, bf16[126,256,256]{2,1,0:T(8,128)(2,1)} %param.37, s32[]{:T(128)S(6)} %select_n.128, bf16[124,256,256]{2,1,0:T(8,128)(2,1)} %param.36, s32[]{:T(128)S(6)} %select_n.126), kind=kOutput, calls=%fused_computation.43 | convolution fusion | flops 134479872 | bytes 1572872 | tf_op jit(solution)/shard_map/dot_general | solution.py:92
  79.3 1.5 %fusion.24 = f32[256,512]{1,0:T(8,128)S(1)} fusion(f32[256,512]{1,0:T(8,128)S(1)} %fusion.23, bf16[256,512]{1,0:T(8,128)(2,1)} %collective-permute-done.3, bf16[126,256,256]{2,1,0:T(8,128)(2,1)} %param.37, s32[]{:T(128)S(6)} %select_n.122, bf16[124,256,256]{2,1,0:T(8,128)(2,1)} %param.36, s32[]{:T(128)S(6)} %select_n.120), kind=kOutput, calls=%fused_computation.44 | convolution fusion | flops 134479872 | bytes 1572872 | tf_op jit(solution)/shard_map/dot_general | solution.py:92
  80.9 1.6 %fusion.25 = f32[512,256]{1,0:T(8,128)S(1)} fusion(f32[256,512]{1,0:T(8,128)S(1)} %fusion.24, bf16[256,512]{0,1:T(8,128)(2,1)} %collective-permute-done.2, bf16[1,256,256]{2,1,0:T(8,128)(2,1)} %param.33, bf16[126,256,256]{2,1,0:T(8,128)(2,1)} %param.37, s32[]{:T(128)S(6)} %select_n.119), kind=kOutput, calls=%fused_computation.45 | convolution fusion | flops 134479872 | bytes 1572868 | tf_op jit(solution)/shard_map/dot_general | solution.py:92
  82.5 1.5 %convolution_bitcast_fusion.3 = f32[2,128,512]{1,2,0:T(8,128)S(1)} fusion(bf16[2,128,256]{2,1,0:T(8,128)(2,1)} %param.30, f32[512,256]{1,0:T(8,128)S(1)} %fusion.25, bf16[256,512]{0,1:T(8,128)(2,1)} %collective-permute-done, bf16[1,256,256]{2,1,0:T(8,128)(2,1)} %param.34), kind=kOutput, calls=%fused_computation.10 | convolution fusion | flops 134479872 | bytes 1572864 | tf_op jit(solution)/shard_map/nekq,nqc->nekc/dot_general | solution.py:31
  84.0 1.4 %fusion.29 = f32[2,512,2,128]{3,1,2,0:T(8,128)S(1)} fusion(bf16[2,2,128,128]{3,2,1,0:T(8,128)(2,1)} %bitcast.231, f32[2,128,512]{1,2,0:T(8,128)S(1)} %convolution_bitcast_fusion.3, bf16[2,128,512]{1,2,0:T(8,128)(2,1)S(1)} %copy-done.4, bf16[2,128,128]{2,1,0:T(8,128)(2,1)} %param.31), kind=kOutput, calls=%fused_computation.51 | convolution fusion | flops 100925440 | bytes 2031616 | tf_op jit(solution)/shard_map/nekq,nqc->nekc/dot_general | solution.py:31
  85.3 0.3 copy.24
  85.7 1.6 %fusion.28 = f32[4,512,2,64]{1,3,2,0:T(8,128)S(1)} fusion(bf16[4,2,64,128]{3,2,1,0:T(8,128)(2,1)} %bitcast.232, f32[4,128,512]{2,1,0:T(8,128)S(1)} %copy.24, bf16[4,128,512]{1,2,0:T(8,128)(2,1)} %bitcast.230, bf16[4,128,128]{2,1,0:T(8,128)(2,1)} %param.28), kind=kOutput, calls=%fused_computation.50 | convolution fusion | flops 134742016 | bytes 2883584 | tf_op jit(solution)/shard_map/nekq,nqc->nekc/dot_general | solution.py:31
  87.3 5.3 %bitcast_add_fusion = f32[8,256,512]{2,1,0:T(8,128)} fusion(f32[8,256,512]{2,1,0:T(8,128)} %fusion.122, bf16[8,256,64]{1,2,0:T(8,128)(2,1)} %param.21, f32[8,64,512]{2,1,0:T(8,128)S(1)} %bitcast.226, bf16[8,64,64]{2,1,0:T(8,128)(2,1)S(1)} %copy-done.5, bf16[8,64,512]{2,1,0:T(8,128)(2,1)} %bitcast.229), kind=kOutput, calls=%fused_computation | convolution fusion | flops 169345024 | bytes 10289152 | tf_op jit(solution)/shard_map/lmk,lkc->lmc/dot_general | solution.py:97
  (19 shorter events, 0.1 us)
Async XLA Ops:
  0.0 66.5 %copy-start = (bf16[8,256,256]{2,1,0:T(8,128)(2,1)S(1)}, bf16[8,256,256]{2,1,0:T(8,128)(2,1)}, u32[]{:S(2)}) copy-start(bf16[8,256,256]{2,1,0:T(8,128)(2,1)} %param.20) | copy-start | bytes 3145732
  0.0 7.7 %copy-start.7 = (bf16[2,128,256]{2,1,0:T(8,128)(2,1)S(1)}, bf16[2,128,256]{2,1,0:T(8,128)(2,1)}, u32[]{:S(2)}) copy-start(bf16[2,128,256]{2,1,0:T(8,128)(2,1)} %param.29) | copy-start | bytes 393220
  0.0 8.1 %copy-start.6 = (bf16[1,256,256]{2,1,0:T(8,128)(2,1)S(1)}, bf16[1,256,256]{2,1,0:T(8,128)(2,1)}, u32[]{:S(2)}) copy-start(bf16[1,256,256]{2,1,0:T(8,128)(2,1)} %param.32) | copy-start | bytes 393220
  4.0 1.6 %copy-start.2 = (bf16[8,64,512]{2,1,0:T(8,128)(2,1)}, bf16[8,64,512]{2,1,0:T(8,128)(2,1)S(1)}, u32[]{:S(2)}) copy-start(bf16[8,64,512]{2,1,0:T(8,128)(2,1)S(1)} %convolution_convert_fusion) | copy-start | bytes 1572868
  5.7 0.8 copy-start.1
  8.1 4.0 %copy-start.3 = (bf16[256,512]{0,1:T(8,128)(2,1)}, bf16[256,512]{0,1:T(8,128)(2,1)S(1)}, u32[]{:S(2)}) copy-start(bf16[256,512]{0,1:T(8,128)(2,1)S(1)} %fusion.36) | copy-start | bytes 786436
  8.4 3.0 %collective-permute-start.1 = (f32[256,512]{0,1:T(8,128)S(1)}, f32[256,512]{0,1:T(8,128)S(1)}, u32[]{:S(2)}, u32[]{:S(2)}) collective-permute-start(f32[256,512]{0,1:T(8,128)S(1)} %convolution_bitcast_fusion.4), channel_id=1, source_target_pairs={{0,1},{1,0},{2,3},{3,2},{4,5},{5,4},{6,7},{7,6},{8,9},{9,8},{10,11... | collective-permute-start | bytes 1572872 | tf_op jit(solution)/shard_map/ppermute | solution.py:78
  12.1 7.6 %collective-permute-start.2 = (bf16[256,512]{0,1:T(8,128)(2,1)}, bf16[256,512]{0,1:T(8,128)(2,1)}, u32[]{:S(2)}, u32[]{:S(2)}) collective-permute-start(bf16[256,512]{0,1:T(8,128)(2,1)} %add_convert_fusion), channel_id=1, source_target_pairs={{0,2},{1,3},{2,0},{3,1},{4,6},{5,7},{6,4},{7,5},{8,10},{9,11},{10,... | collective-permute-start | bytes 786440 | tf_op jit(solution)/shard_map/ppermute | solution.py:69
  23.0 8.4 %collective-permute-start.3 = (bf16[256,512]{1,0:T(8,128)(2,1)}, bf16[256,512]{1,0:T(8,128)(2,1)}, u32[]{:S(2)}, u32[]{:S(2)}) collective-permute-start(bf16[256,512]{1,0:T(8,128)(2,1)} %fusion.8), channel_id=1, source_target_pairs={{0,4},{1,5},{2,6},{3,7},{4,0},{5,1},{6,2},{7,3},{8,12},{9,13},{10,... | collective-permute-start | bytes 786440 | tf_op jit(solution)/shard_map/ppermute | solution.py:69
  33.3 5.8 %collective-permute-start.4 = (bf16[256,512]{1,0:T(8,128)(2,1)}, bf16[256,512]{1,0:T(8,128)(2,1)}, u32[]{:S(2)}, u32[]{:S(2)}) collective-permute-start(bf16[256,512]{1,0:T(8,128)(2,1)} %fusion.10), channel_id=1, source_target_pairs={{0,8},{1,9},{2,10},{3,11},{4,12},{5,13},{6,14},{7,15},{8,0},{9,1},... | collective-permute-start | bytes 786440 | tf_op jit(solution)/shard_map/ppermute | solution.py:69
  41.1 46.2 %copy-start.5 = (bf16[8,64,64]{2,1,0:T(8,128)(2,1)S(1)}, bf16[8,64,64]{2,1,0:T(8,128)(2,1)}, u32[]{:S(2)}) copy-start(bf16[8,64,64]{2,1,0:T(8,128)(2,1)} %param.25) | copy-start | bytes 196612
  41.1 6.8 %collective-permute-start.5 = (bf16[256,512]{1,0:T(8,128)(2,1)}, bf16[256,512]{1,0:T(8,128)(2,1)}, u32[]{:S(2)}, u32[]{:S(2)}) collective-permute-start(bf16[256,512]{1,0:T(8,128)(2,1)} %fusion.12), channel_id=1, source_target_pairs={{0,16},{1,17},{2,18},{3,19},{4,20},{5,21},{6,22},{7,23},{8,24},{9,... | collective-permute-start | bytes 786440 | tf_op jit(solution)/shard_map/ppermute | solution.py:69
  49.9 11.9 %collective-permute-start.6 = (bf16[256,512]{1,0:T(8,128)(2,1)}, bf16[256,512]{1,0:T(8,128)(2,1)}, u32[]{:S(2)}, u32[]{:S(2)}) collective-permute-start(bf16[256,512]{1,0:T(8,128)(2,1)} %fusion.14), channel_id=1, source_target_pairs={{0,32},{1,33},{2,34},{3,35},{4,36},{5,37},{6,38},{7,39},{8,40},{9,... | collective-permute-start | bytes 786440 | tf_op jit(solution)/shard_map/ppermute | solution.py:69
  51.6 30.9 %collective-permute-start = (bf16[256,512]{0,1:T(8,128)(2,1)}, bf16[256,512]{0,1:T(8,128)(2,1)}, u32[]{:S(2)}, u32[]{:S(2)}) collective-permute-start(bf16[256,512]{0,1:T(8,128)(2,1)} %copy-done.3), channel_id=1, source_target_pairs={{0,1},{1,0},{2,3},{3,2},{4,5},{5,4},{6,7},{7,6},{8,9},{9,8},{10,11... | collective-permute-start | bytes 786440 | tf_op jit(solution)/shard_map/ppermute | solution.py:69
  56.7 27.3 %copy-start.4 = (bf16[2,128,512]{1,2,0:T(8,128)(2,1)S(1)}, bf16[2,128,512]{1,2,0:T(8,128)(2,1)}, u32[]{:S(2)}) copy-start(bf16[2,128,512]{1,2,0:T(8,128)(2,1)} %reshape.76) | copy-start | bytes 786436
  63.1 10.2 %collective-permute-start.7 = (bf16[256,512]{1,0:T(8,128)(2,1)S(1)}, bf16[256,512]{1,0:T(8,128)(2,1)}, u32[]{:S(2)}, u32[]{:S(2)}) collective-permute-start(bf16[256,512]{1,0:T(8,128)(2,1)S(1)} %fusion.16), channel_id=1, source_target_pairs={{0,64},{1,65},{2,66},{3,67},{4,68},{5,69},{6,70},{7,71},{8,72},{9,... | collective-permute-start | bytes 786440 | tf_op jit(solution)/shard_map/ppermute | solution.py:69
where the time goes:
time: 93.2 us; the launch traced here: 92.6 us
  matrix products  41.9 us (45%)
  waiting for transfers between devices  21.6 us (23%)
  starting transfers between devices  19.6 us (21%)
  local copies, waits for them, and re-layouts  5.7 us (6%)
  other arithmetic  3.54 us (4%)
    ppermute x7, waiting for transfers between devices, body(): sib_x = lax.ppermute(node_x, 'tree', pair_list)  20 us
    ppermute x7, starting transfers between devices, body(): sib_x = lax.ppermute(node_x, 'tree', pair_list)  18.2 us
    dot_general x6, matrix products, body(): jnp.dot(r_here, y_node, preferred_element_type=jnp.float32)  9.17 us
    dot_general x5, matrix products, body(): jnp.einsum('kq,kc->qc', pick_node(w_top, 2 ** level - 4 + sib_idx), sib_x...  8.51 us
    dot_general x5, matrix products, body(): jnp.einsum('kq,kc->qc', pick_node(w_top, 2 ** level - 4 + node_idx), node...  7.06 us
    dot_general x1, matrix products, body(): jnp.einsum('lmk,lkc->lmc', u_leaf, y_skel, preferred_element_type=jnp.flo...  5.28 us
    dot_general x3, matrix products, push_local(): jnp.einsum('nekq,nqc->nekc', r_pairs, y_parent, preferred_element_type=jn...  4.45 us
    rev x2, local copies, waits for them, and re-layouts, couple_local(): swapped = jnp.flip(pairs, axis=1).reshape(x_level.shape)  3.82 us
  transfers between devices with their start and end apart: 8, of which 6 were waited for; matrix products, arithmetic and copies ran while one was open for 25% of the time, Pallas kernels for 0%

commit v1 on v0

v1 whole, which is shorter than its diff:
```python
import jax
import jax.numpy as jnp
from jax import lax
from jax.experimental import pallas as pl
from jax.experimental.pallas import tpu as pltpu
from jax.sharding import PartitionSpec as P

F32 = jnp.float32
BF16 = jnp.bfloat16
MESH = pl.DeviceIdType.MESH
COLS = 64


def nn(a, b):
    return lax.dot_general(a, b, (((1,), (0,)), ((), ())), preferred_element_type=F32)


def nt(a, b):
    return lax.dot_general(a, b, (((1,), (1,)), ((), ())), preferred_element_type=F32)


def tn(a, b):
    return lax.dot_general(a, b, (((0,), (0,)), ((), ())), preferred_element_type=F32)


def kernel(x, d, u, v, w0, r0, b0, w1, r1, b1, w2, r2, b2, wu, ru, bu, wt, rt, bt, out,
           xf, xb, dv, uv, vv, w0v, r0v, b0v, w1v, r1v, b1v, w2v, r2v, b2v, wuv, ruv, buv,
           wt6, wt5, wt4, wt3, wt2, rt6, rt5, rt4, rt3, rt2, bt6, bt5, bt4, bt3, bt2, bt1,
           xh0, xh1, xh2, x7, x7s, part, partr, x6h, buf6, x5, x4s, buf4, x3, x2s, buf2, x1,
           g0, g1, g2, g7, g6t, g5t, y6h, yfull, yh0,
           xsem, lsem, wsem, s0, q0, s6, q6, s4, q4, s2, q2, sy, qy, sc, qc):
    me = lax.axis_index('tree')
    core = me % 2
    px = (me // 2) % 4
    py = (me // 8) % 4
    pz = me // 32
    line = me // 8
    partner = me + 1 - 2 * core

    def at_x(i):
        return me + 2 * (i - px)

    def at_y(i):
        return me + 8 * (i - py)

    def at_z(i):
        return me + 32 * (i - pz)

    xcopies = [pltpu.make_async_copy(x.at[pl.ds(256 * i, 256)], xf.at[pl.ds(256 * i, 256)], xsem.at[i]) for i in range(8)]
    early = [(v, vv), (w0, w0v), (w1, w1v), (w2, w2v), (wu, wuv)]
    late = [
        (bu, buv), (b0, b0v), (b1, b1v), (b2, b2v),
        (wt.at[pl.ds(60 + 4 * line, 4)], wt6), (wt.at[pl.ds(28 + 2 * line, 2)], wt5),
        (wt.at[pl.ds(12 + 4 * pz, 4)], wt4), (wt.at[pl.ds(4 + 2 * pz, 2)], wt3), (wt.at[pl.ds(0, 4)], wt2),
        (bt.at[pl.ds(62 + 4 * line, 4)], bt6), (bt.at[pl.ds(30 + 2 * line, 2)], bt5),
        (bt.at[pl.ds(14 + line, 1)], bt4), (bt.at[pl.ds(6 + line // 2, 1)], bt3),
        (bt.at[pl.ds(2 + pz, 1)], bt2), (bt.at[pl.ds(pz // 2, 1)], bt1),
        (rt.at[pl.ds(60 + 4 * line, 4)], rt6), (rt.at[pl.ds(28 + 2 * line, 2)], rt5),
        (rt.at[pl.ds(12 + line, 1)], rt4), (rt.at[pl.ds(4 + line // 2, 1)], rt3), (rt.at[pl.ds(pz, 1)], rt2),
        (d, dv), (ru, ruv), (r2, r2v), (r1, r1v), (r0, r0v), (u, uv),
    ]
    ecopies = [pltpu.make_async_copy(a, b, lsem.at[i]) for i, (a, b) in enumerate(early)]
    lcopies = [pltpu.make_async_copy(a, b, wsem.at[i]) for i, (a, b) in enumerate(late)]
    ecopies[0].start()
    for c in xcopies:
        c.start()
    for c in ecopies[1:]:
        c.start()
    for c in lcopies:
        c.start()

    peers = [partner]
    for k in range(1, 4):
        peers += [at_x((px + k) % 4), at_y((py + k) % 4), at_z((pz + k) % 4)]
    barrier = pltpu.get_barrier_semaphore()
    for p in peers:
        pl.semaphore_signal(barrier, inc=1, device_id={'tree': p}, device_id_type=MESH)

    def send(src, dst, ssem, rsem, dev):
        c = pltpu.make_async_remote_copy(src_ref=src, dst_ref=dst, send_sem=ssem, recv_sem=rsem, device_id={'tree': dev}, device_id_type=MESH)
        c.start()
        return c

    ecopies[0].wait()
    for i in range(8):
        xcopies[i].wait()
        rows = pl.ds(256 * i, 256)
        xi = xf[rows, :].astype(BF16)
        xb[rows, :] = xi
        xh0[pl.ds(64 * i, 64), :] = nn(vv[i], xi).astype(BF16)
    for c in ecopies[1:]:
        c.wait()
    for n in range(4):
        xh1[pl.ds(128 * n, 128), :] = tn(w0v[2 * n:2 * n + 2].reshape(128, 128), xh0[pl.ds(128 * n, 128), :]).astype(BF16)
    for n in range(2):
        xh2[pl.ds(128 * n, 128), :] = tn(w1v[2 * n:2 * n + 2].reshape(256, 128), xh1[pl.ds(256 * n, 256), :]).astype(BF16)
    x7v = tn(w2v[...].reshape(256, 256), xh2[...]).astype(BF16)
    x7[0] = x7v[:, :256]
    x7[1] = x7v[:, 256:]

    part[...] = tn(x7[1 - core], wuv[0])
    pl.semaphore_wait(barrier, 10)
    c_part = send(part, partr, s0.at[0], q0.at[0], partner)
    c_skel = send(x7, x7s, s0.at[1], q0.at[1], partner)
    own = tn(x7[core], wuv[0])
    for c in lcopies:
        c.wait()
    c_part.wait_recv()
    x6h[...] = (own + partr[...]).astype(BF16).reshape(4, COLS, 256)

    c6 = [send(x6h.at[(px + k) % 4], buf6.at[px], s6.at[k - 1], q6.at[px], at_x((px + k) % 4)) for k in range(1, 4)]
    buf6[px] = x6h[px]

    def got(buf, sem, k, pos):
        src = (pos + k) % 4
        pltpu.make_async_remote_copy(src_ref=buf.at[src], dst_ref=buf.at[src], send_sem=sem.at[src], recv_sem=sem.at[src], device_id={'tree': partner}, device_id_type=MESH).wait_recv()

    for i in range(8):
        g0[pl.ds(64 * i, 64), :] = nn(b0v[i], xh0[pl.ds(64 * (i ^ 1), 64), :])
    for n in range(4):
        g1[pl.ds(128 * n, 128), :] = nn(b1v[n], xh1[pl.ds(128 * (n ^ 1), 128), :])
    for n in range(2):
        g2[pl.ds(128 * n, 128), :] = nn(b2v[n], xh2[pl.ds(128 * (1 - n), 128), :])

    def near(lo, hi):
        def step(i, carry):
            rows = pl.ds(pl.multiple_of(256 * i, 256), 256)
            out[rows, :] = nn(dv[i], xb[rows, :])
            return carry
        lax.fori_loop(lo, hi, step, 0)

    near(0, 3)
    for k in range(1, 4):
        got(buf6, q6, k, px)
    for j in range(2):
        x5[j] = (nn(buf6[2 * j], wt6[2 * j]) + nn(buf6[2 * j + 1], wt6[2 * j + 1])).astype(BF16)
    x4s[...] = (nn(x5[0], wt5[0]) + nn(x5[1], wt5[1])).astype(BF16)

    c4 = [send(x4s, buf4.at[py], s4.at[k - 1], q4.at[py], at_y((py + k) % 4)) for k in range(1, 4)]
    buf4[py] = x4s[...]
    for i in range(4):
        g6t[i] = nt(buf6[i ^ 1], bt6[i])
    for j in range(2):
        g5t[j] = nt(x5[1 - j], bt5[j])
    c_skel.wait_recv()
    for h in range(2):
        g7[:, pl.ds(256 * h, 256)] = nn(buv[0], x7s[h])
    near(3, 6)
    for k in range(1, 4):
        got(buf4, q4, k, py)
    for j in range(2):
        x3[j] = (nn(buf4[2 * j], wt4[2 * j]) + nn(buf4[2 * j + 1], wt4[2 * j + 1])).astype(BF16)
    x2s[...] = (nn(x3[0], wt3[0]) + nn(x3[1], wt3[1])).astype(BF16)

    c2 = [send(x2s, buf2.at[pz], s2.at[k - 1], q2.at[pz], at_z((pz + k) % 4)) for k in range(1, 4)]
    buf2[pz] = x2s[...]
    g4t = nt(buf4[py + 1 - 2 * (py % 2)], bt4[0])
    g3t = nt(x3[1 - py // 2], bt3[0])
    near(6, 8)
    for k in range(1, 4):
        got(buf2, q2, k, pz)
    for j in range(2):
        x1[j] = (nn(buf2[2 * j], wt2[2 * j]) + nn(buf2[2 * j + 1], wt2[2 * j + 1])).astype(BF16)
    g2t = nt(buf2[pz + 1 - 2 * (pz % 2)], bt2[0])

    y1 = nt(x1[1 - pz // 2], bt1[0]).astype(BF16)
    y2 = (g2t + nt(y1, rt2[0])).astype(BF16)
    y3 = (g3t + nt(y2, rt3[0])).astype(BF16)
    y4 = (g4t + nt(y3, rt4[0])).astype(BF16)
    y5 = [(g5t[j] + nt(y4, rt5[j])).astype(BF16) for j in range(2)]
    for i in range(4):
        y6h[i] = (g6t[i] + nt(y5[i // 2], rt6[i])).astype(BF16)

    cy = [send(y6h.at[(px + k) % 4], yfull.at[4 * core + px], sy.at[k - 1], qy.at[px], at_x((px + k) % 4)) for k in range(1, 4)]
    cc = [send(y6h.at[px], yfull.at[4 * core + px], sc.at[px], qc.at[px], partner)]
    yfull[4 * core + px] = y6h[px]
    for k in range(1, 4):
        src = (px + k) % 4
        slot = yfull.at[4 * core + src]
        pltpu.make_async_remote_copy(src_ref=slot, dst_ref=slot, send_sem=qy.at[src], recv_sem=qy.at[src], device_id={'tree': partner}, device_id_type=MESH).wait_recv()
        cc.append(send(slot, slot, sc.at[src], qc.at[src], partner))
    for i in range(4):
        slot = yfull.at[4 * (1 - core) + i]
        pltpu.make_async_remote_copy(src_ref=slot, dst_ref=slot, send_sem=qc.at[i], recv_sem=qc.at[i], device_id={'tree': partner}, device_id_type=MESH).wait_recv()

    y7 = (g7[...] + nt(ruv[0], yfull[...].reshape(512, 256))).astype(BF16)
    yh2 = [(g2[pl.ds(128 * n, 128), :] + nn(r2v[n], y7)).astype(BF16) for n in range(2)]
    yh1 = [(g1[pl.ds(128 * n, 128), :] + nn(r1v[n], yh2[n // 2])).astype(BF16) for n in range(4)]
    for i in range(8):
        yi = (g0[pl.ds(64 * i, 64), :] + nn(r0v[i], yh1[i // 2])).astype(BF16)
        out[pl.ds(256 * i, 256), :] += tn(uv[i], yi)

    for c in [c_part, c_skel] + c6 + c4 + c2 + cy + cc:
        c.wait_send()


def solution(mesh):
    rows_spec = P(('batch', 'tree'), None)
    tree_spec = P('tree', None, None)
    full_spec = P(None, None, None)

    def body(*args):
        args = list(args)
        for i in (2, 3):
            args[i] = jnp.swapaxes(args[i], 1, 2)
        args = [pltpu.with_memory_space_constraint(a, pltpu.HBM) for a in args]
        shapes = [a.shape for a in args]
        rows, cols = shapes[0]

        def b16(*shape):
            return pltpu.VMEM(shape, BF16)

        def f32(*shape):
            return pltpu.VMEM(shape, F32)

        dma = pltpu.SemaphoreType.DMA
        mat = (256, 256)
        scratch = [f32(rows, cols)] + [b16(rows, cols)] + [b16(*s) for s in shapes[1:16]]
        scratch += [b16(n, *mat) for n in (4, 2, 4, 2, 4, 4, 2, 1, 1, 1, 4, 2, 1, 1, 1, 1)]
        scratch += [b16(512, cols), b16(512, cols), b16(256, cols), b16(2, *mat), b16(2, *mat), f32(*mat), f32(*mat)]
        line = b16(4, COLS, 256)
        scratch += [line, line, b16(2, COLS, 256), b16(COLS, 256), line, b16(2, COLS, 256), b16(COLS, 256), line, b16(2, COLS, 256)]
        scratch += [f32(512, cols), f32(512, cols), f32(256, cols), f32(256, cols), f32(4, COLS, 256), f32(2, COLS, 256), line, b16(8, COLS, 256), b16(512, cols)]
        scratch += [dma((8,)), dma((5,)), dma((26,)), dma((2,)), dma((2,))]
        scratch += [dma((3,)), dma((4,))] * 4 + [dma((4,)), dma((4,))]
        return pl.pallas_call(
            kernel,
            out_shape=jax.ShapeDtypeStruct((rows, cols), F32),
            in_specs=[pl.BlockSpec(memory_space=pltpu.HBM)] * len(args),
            out_specs=pl.BlockSpec(memory_space=pltpu.VMEM),
            scratch_shapes=scratch,
            compiler_params=pltpu.CompilerParams(collective_id=0, has_side_effects=True, vmem_limit_bytes=40 * 1024 * 1024),
        )(*args)

    return jax.shard_map(body, mesh=mesh, in_specs=(rows_spec,) + (tree_spec,) * 15 + (full_spec,) * 3, out_specs=rows_spec, check_vma=False)
```

time: 93.2 us -> 37.8 us (0.41)
  matrix products: 41.9 us -> 0 us
  Pallas kernels: 0 us -> 35.6 us
  waiting for transfers between devices: 21.6 us -> 0 us
  starting transfers between devices: 19.6 us -> 0 us
  local copies, waits for them, and re-layouts: 5.7 us -> 2.02 us
  other arithmetic: 3.54 us -> 0 us
    dot_general x26 -> x0, matrix products: 41.9 us -> none  [the longest x6 9.17 us: body(): jnp.dot(r_here, y_node, preferred_element_type=jnp.float32)]
    pallas_call x0 -> x1, Pallas kernels: none -> 35.6 us  [body(): pl.pallas_call(kernel, out_shape=jax.ShapeDtypeStruct((rows, cols), F32),...]
    ppermute x8 -> x0, waiting for transfers between devices: 21.6 us -> none  [the longest x7 20 us: body(): sib_x = lax.ppermute(node_x, 'tree', pair_list)]
    ppermute x8 -> x0, starting transfers between devices: 19.6 us -> none  [the longest x7 18.2 us: body(): sib_x = lax.ppermute(node_x, 'tree', pair_list)]
    rev x2 -> x0, local copies, waits for them, and re-layouts: 3.82 us -> none  [couple_local(): swapped = jnp.flip(pairs, axis=1).reshape(x_level.shape)]
    convert_element_type x5 -> x0, other arithmetic: 3.54 us -> none  [the longest x1 2.56 us: body(): x_leaf = x_loc.astype(jnp.bfloat16).reshape(leaves_dev, leaf_size, rhs_cols)]
    unnamed x16 -> x1, local copies, waits for them, and re-layouts: 0.82 us -> 2.02 us
    reshape x2 -> x0, local copies, waits for them, and re-layouts: 1.07 us -> none  [the longest x1 0.74 us: couple_local(): swapped = jnp.flip(pairs, axis=1).reshape(x_level.shape)]
  transfers between devices with their start and end apart: 8 -> 0, of which waited for: 6 -> 0; matrix products, arithmetic and copies ran while one was open for 25% -> 0% of each run, Pallas kernels for 0% -> 0%
where the time goes in v1:
time: 37.8 us; the launch traced here: 37.7 us
  Pallas kernels  35.6 us (94%)
  local copies, waits for them, and re-layouts  2.02 us (5%)
    pallas_call x1, Pallas kernels, body(): pl.pallas_call(kernel, out_shape=jax.ShapeDtypeStruct((rows, cols), F32),...  35.6 us
    unnamed x1, local copies, waits for them, and re-layouts  2.02 us

profile of v1, /device:TPU:1, one launch (start us, length us, event | category | flops | bytes accessed | tf_op | source)
XLA Modules:
  0.0 37.7 jit_solution(17073327916549973385)
XLA Ops:
  0.0 35.6 %shard_map.181 = f32[2048,512]{1,0:T(8,128)S(1)} custom-call(f32[2048,512]{1,0:T(8,128)} %x.1, bf16[8,256,256]{2,1,0:T(8,128)(2,1)} %d.1, bf16[8,64,256]{2,1,0:T(8,128)(2,1)} %bitcast.2, bf16[8,64,256]{2,1,0:T(8,128)(2,1)} %bitcast.3, bf16[8,64,128]{2,1,0:T(8,128)(2,1)} %w0.1, bf16[8,64,128]{2,1,0:T(8,128)(2,1)} %r0.1, bf16[8,64,64]{2,1,0:T(8,128)(2,1)} %b0.1, ...), custom_call_target="tpu_custom_call" | custom-call | tf_op jit(solution)/shard_map/pallas_call | solution.py:226
  35.6 2.0 %copy.21 = f32[2048,512]{1,0:T(8,128)} copy(f32[2048,512]{1,0:T(8,128)S(1)} %shard_map.181) | data formatting | bytes 8388608
